TPU v7x, 32 devices: a whole 2x2x4 slice. The times are simulated.
32 devices in a mesh: tile: 16 (over z, x, core), mem: 2 (over y).
Axes of the slice: x: 2, y: 2, z: 4, core: 2. Of those that a mesh axis runs over, the one named last changes fastest.
Arguments:
- anomalies: bfloat16 [80, 137, 2048], P('mem', None, 'tile'), may hold values from -6 to 6
- analysis_weights: bfloat16 [16, 80, 80], P('tile'), may hold values from -0.6 to 1.7
- background_mean: bfloat16 [137, 2048], P(None, 'tile'), may hold values from -6 to 6
- background: bfloat16 [80, 137, 2048], P('mem', None, 'tile'), may hold values from -6 to 6
- jacobian_table: bfloat16 [8461, 137], replicated, may hold values from -0.5 to 0.5
- channel_list: int32 [96], replicated, may hold values from 0 to 8460
- send_slots: int32 [16, 16, 32], P('tile'), may hold values from -1 to 127, as said below
- footprint: int32 [8192, 4], P('tile'), may hold values from 0 to 511, as said below
- footprint_weight: bfloat16 [8192, 4], P('tile'), may hold values from 0.25 to 1
- channel_bias: float32 [96], replicated, may hold values from -4 to 4
Outputs:
- analysis_members: bfloat16 [80, 137, 2048], P('mem', None, 'tile')
- radiance_prior: float32 [96, 80, 8192], P(None, 'mem', 'tile')
Inputs may be any that keep to these rules, and one draw needn't show every extreme that they name: `send_slots`: entry [s, d, i] is a column within owner s's block of 128 columns that owner s sends to tile d in slot i, or -1 for an empty slot; the filled slots of a pair come first, each pair fills 1 to 32 slots, and in every draw one tile receives 32 filled slots from every owner. `footprint`: entry [o, j] is a slot of the buffer of observation o's tile, which holds 32 slots from each owner in owner order; every entry names a filled slot, the 4 entries of a row differ, and every filled slot is named by some row of that tile.
All inputs are finite; a program needn't handle non-finite values.
Results may differ from a plain program's by a relative error of at most 0.0021.
Values may be sent and summed in bfloat16 or wider, within the bound.
No kernel may reach another device: no remote copies, remote signals or barrier semaphores. Data moves between devices by JAX's collectives and lax.ppermute only.
A program may use at most 128 MiB of HBM per device.

v0:
```python
import jax
import jax.numpy as jnp
from jax import lax
from jax.sharding import PartitionSpec as P

GROUP = 128
FOOT = 4


def shards(
    anomalies,
    analysis_weights,
    background_mean,
    background,
    jacobian_table,
    channel_list,
    send_slots,
    footprint,
    footprint_weight,
    channel_bias,
):
    mem_dev = anomalies.shape[0]
    levels = anomalies.shape[1]
    columns_dev = anomalies.shape[2]
    groups = columns_dev // GROUP
    mean_float = background_mean.astype(jnp.float32)
    member_start = lax.axis_index("mem") * mem_dev
    member_piece = lax.all_gather(anomalies, "mem", axis=0, tiled=True)
    piece_rows = member_piece.shape[0]
    weight_rows = analysis_weights
    weight_rows = lax.dynamic_slice_in_dim(weight_rows, member_start, mem_dev, 2)
    reshaped = member_piece.reshape(piece_rows, levels, groups, GROUP)
    mixture = jnp.einsum(
        "klgc,gkm->mlgc", reshaped, weight_rows, preferred_element_type=jnp.float32
    )
    analysis_members = (mixture.reshape(mem_dev, levels, columns_dev) + mean_float[None]).astype(
        jnp.bfloat16
    )
    selected = jnp.take(jacobian_table, channel_list, axis=0)
    slot_cols = jnp.maximum(send_slots[0], 0).reshape(-1)
    owned = jnp.einsum(
        "cl,klx->ckx", selected, background, preferred_element_type=jnp.float32
    ).astype(jnp.bfloat16)
    packed = jnp.take(owned, slot_cols, axis=2)
    received = lax.all_to_all(packed, "tile", split_axis=2, concat_axis=2, tiled=True)
    channels = received.shape[0]
    obs_count = footprint.shape[0]
    picked = jnp.take(received, footprint.reshape(-1), axis=2).reshape(
        channels, mem_dev, obs_count, FOOT
    )
    weighted = picked.astype(jnp.float32) * footprint_weight.astype(jnp.float32)[None, None]
    prior_out = jnp.sum(weighted, axis=3) + channel_bias[:, None, None]
    return (analysis_members, prior_out)


def solution(mesh):
    placed = (
        P("mem", None, "tile"),
        P("tile", None, None),
        P(None, "tile"),
        P("mem", None, "tile"),
        P(),
        P(),
        P("tile", None, None),
        P("tile", None),
        P("tile", None),
        P(),
    )
    return jax.shard_map(
        shards,
        mesh=mesh,
        in_specs=placed,
        out_specs=(P("mem", None, "tile"), P(None, "mem", "tile")),
        check_vma=False,
    )
```

profile of v0, /device:TPU:11, one launch (start us, length us, event | category | flops | bytes accessed | tf_op | source)
XLA Modules:
  0.0 223.6 jit_solution(4446422956958889436)
XLA Ops:
  7.2 0.0 copy-start
  7.2 0.8 compare_and_fusion.1
  8.0 0.7 compare_select_fusion.2
  8.6 0.7 broadcast_compare_fusion
  9.3 0.7 broadcast_maximum_fusion
  10.0 0.1 le.39
  10.1 0.1 reshape.96
  10.2 5.6 %copy.28 = bf16[8461,137]{1,0:T(8,128)(2,1)} copy(bf16[8461,137]{0,1:T(8,128)(2,1)} %param.14) | data formatting | bytes 4636628 | tf_op args[4]
  15.8 3.5 %gather_fusion = bf16[96,137]{1,0:T(8,128)(2,1)S(1)} fusion(bf16[8461,137]{1,0:T(8,128)(2,1)} %copy.28, s32[1024]{0:T(1024)S(1)} %pad_clamp_fusion.1), kind=kCustom, calls=%fused_computation | custom fusion | bytes 52992 | tf_op jit(solution)/shard_map/jit(_take)/gather | solution.py:39
  19.2 0.0 copy-done
  19.3 0.5 fusion.2
  19.7 1.4 copy.31
  21.2 4.0 %gather_fusion.1 = bf16[512,96,40]{1,2,0:T(8,128)(2,1)} fusion(bf16[96,40,128]{0,1,2:T(8,128)(2,1)S(1)} %copy.31, s32[1024]{0:T(1024)S(1)} %pad_clamp_fusion), kind=kCustom, calls=%fused_computation.1 | custom fusion | bytes 7866368 | tf_op jit(solution)/shard_map/jit(_take)/gather | solution.py:44
  25.1 6.6 %select_bitcast_fusion = bf16[96,40,512]{0,1,2:T(8,128)(2,1)} fusion(bf16[512,96,40]{1,2,0:T(8,128)(2,1)} %gather_fusion.1, pred[512]{0:T(512)(128)(4,1)S(1)} %le.39), kind=kLoop, calls=%fused_computation.4 | loop fusion | flops 1966080 | bytes 7864832 | tf_op jit(solution)/shard_map/jit(_take)/select_n | solution.py:44
  31.7 6.7 %all-to-all-start = ((bf16[96,40,512]{0,1,2:T(8,128)(2,1)}), bf16[96,40,512]{0,1,2:T(8,128)(2,1)}, u32[]{:S(2)}, u32[]{:S(2)}) async-start(bf16[96,40,512]{0,1,2:T(8,128)(2,1)} %select_bitcast_fusion), calls=%async_computation | async-start | bytes 10485760 | tf_op jit(solution)/shard_map/all_to_all | solution.py:45
  38.4 0.0 all-gather.2.cloned.1.call-start
  38.5 0.7 all-gather.2.cloned.1.call-update
  39.1 0.0 copy-done.3
  39.2 0.1 copy.32
  39.3 0.2 copy.27
  39.5 0.0 copy-done.2
  39.5 0.0 copy-done.5
  39.6 0.1 copy.33
  39.7 0.2 reshape.85
  39.9 42.4 %all-gather.2.cloned.1.call-done = bf16[80,137,128]{2,0,1:T(8,128)(2,1)} async-done(((bf16[40,137,128]{2,0,1:T(8,128)(2,1)}), bf16[80,137,128]{2,0,1:T(8,128)(2,1)}) %all-gather.2.cloned.1.call-update) | async-done | bytes 2805776 | tf_op jit(solution)/shard_map/all_gather | solution.py:28
  82.3 0.0 copy-done.4
  82.3 3.5 %add_convert_fusion = bf16[40,137,128]{2,0,1:T(8,128)(2,1)} fusion(bf16[80,137,128]{2,0,1:T(8,128)(2,1)} %all-gather.2.cloned.1.call-done, f32[137,128]{1,0:T(8,128)S(1)} %convert_element_type.15, bf16[1,80,80]{2,1,0:T(8,128)(2,1)S(1)} %copy-done.4, s32[]{:T(128)S(6)} %select_n.44), kind=kOutput, calls=%fused_computation.6 | convolution fusion | flops 113633280 | bytes 4291588 | tf_op jit(solution)/shard_map/klgc,gkm->mlgc/dot_general | solution.py:33
  85.9 67.5 %all-to-all-done = bf16[96,40,512]{0,1,2:T(8,128)(2,1)} async-done(((bf16[96,40,512]{0,1,2:T(8,128)(2,1)}), bf16[96,40,512]{0,1,2:T(8,128)(2,1)}, u32[]{:S(2)}, u32[]{:S(2)}) %all-to-all-start) | async-done | bytes 3932192 | tf_op jit(solution)/shard_map/all_to_all | solution.py:45
  153.3 24.0 %gather_fusion.2 = bf16[2048,96,40]{1,2,0:T(8,128)(2,1)} fusion(bf16[96,40,512]{0,1,2:T(8,128)(2,1)} %all-to-all-done, s32[2048]{0:T(1024)S(1)} %broadcast_clamp_fusion), kind=kCustom, calls=%fused_computation.2 | custom fusion | bytes 31465472 | tf_op jit(solution)/shard_map/jit(_take)/gather | solution.py:48
  177.3 19.8 %multiply_reduce_fusion = f32[96,40,512]{0,1,2:T(8,128)} fusion(f32[512,4]{1,0:T(8,128)S(1)} %copy.33, pred[512,4]{1,0:T(8,128)(4,1)S(1)} %copy.27, bf16[2048,96,40]{1,2,0:T(8,128)(2,1)} %gather_fusion.2), kind=kLoop, calls=%fused_computation.3 | loop fusion | flops 29491200 | bytes 23603200 | tf_op jit(solution)/shard_map/reduce_sum | solution.py:52
  197.2 8.7 %broadcast_add_fusion = f32[96,40,512]{0,1,2:T(8,128)} fusion(f32[96,40,512]{0,1,2:T(8,128)} %multiply_reduce_fusion, f32[96]{0:T(128)S(1)} %copy-done.6), kind=kLoop, calls=%fused_computation.5 | loop fusion | flops 1966080 | bytes 15729024 | tf_op jit(solution)/shard_map/add | solution.py:52
  205.9 10.8 %copy.34 = f32[96,40,512]{2,1,0:T(8,128)} copy(f32[96,40,512]{0,1,2:T(8,128)} %broadcast_add_fusion) | data formatting | bytes 15728640
  (14 shorter events, 0.1 us)
Async XLA Ops:
  7.2 12.1 %copy-start = (bf16[40,137,128]{2,0,1:T(8,128)(2,1)S(1)}, bf16[40,137,128]{2,0,1:T(8,128)(2,1)}, u32[]{:S(2)}) copy-start(bf16[40,137,128]{2,0,1:T(8,128)(2,1)} %param.13) | copy-start | bytes 4208644
  31.7 7.4 %copy-start.3 = (s32[512,4]{0,1:T(4,128)S(1)}, s32[512,4]{0,1:T(4,128)}, u32[]{:S(2)}) copy-start(s32[512,4]{0,1:T(4,128)} %param.17) | copy-start | bytes 24580
  31.7 7.8 %copy-start.2 = (bf16[137,128]{1,0:T(8,128)(2,1)S(1)}, bf16[137,128]{1,0:T(8,128)(2,1)}, u32[]{:S(2)}) copy-start(bf16[137,128]{1,0:T(8,128)(2,1)} %param.12) | copy-start | bytes 105220
  31.7 7.8 %copy-start.5 = (bf16[512,4]{0,1:T(4,128)(2,1)S(1)}, bf16[512,4]{0,1:T(4,128)(2,1)}, u32[]{:S(2)}) copy-start(bf16[512,4]{0,1:T(4,128)(2,1)} %param.18) | copy-start | bytes 12292
  31.7 50.6 %copy-start.4 = (bf16[1,80,80]{2,1,0:T(8,128)(2,1)S(1)}, bf16[1,80,80]{2,1,0:T(8,128)(2,1)}, u32[]{:S(2)}) copy-start(bf16[1,80,80]{2,1,0:T(8,128)(2,1)} %param.11) | copy-start | bytes 38404
  31.7 121.6 %all-to-all-start = ((bf16[96,40,512]{0,1,2:T(8,128)(2,1)}), bf16[96,40,512]{0,1,2:T(8,128)(2,1)}, u32[]{:S(2)}, u32[]{:S(2)}) async-start(bf16[96,40,512]{0,1,2:T(8,128)(2,1)} %select_bitcast_fusion), calls=%async_computation | async-start | bytes 10485760 | tf_op jit(solution)/shard_map/all_to_all | solution.py:45
  38.4 43.9 %all-gather.2.cloned.1.call-start = ((), (), s32[]{:S(2)}) async-start(), calls=%async_computation.1 | async-start | bytes 4208640 | tf_op jit(solution)/shard_map/all_gather | solution.py:28
  177.3 19.9 %copy-start.6 = (f32[96]{0:T(128)S(1)}, f32[96]{0:T(128)}, u32[]{:S(2)}) copy-start(f32[96]{0:T(128)} %param.19) | copy-start | bytes 1156
  197.2 19.6 %copy-start.1 = (bf16[40,137,128]{2,0,1:T(8,128)(2,1)S(1)}, bf16[40,137,128]{2,0,1:T(8,128)(2,1)}, u32[]{:S(2)}) copy-start(bf16[40,137,128]{2,0,1:T(8,128)(2,1)} %param.13) | copy-start | bytes 4208644
Sparse Core Ops, SparseCore 0:
  40.8 41.5 all-gather.1
where the time goes:
time: 224 us
  waiting for transfers between devices  111 us (50%)
  local copies, waits for them, and re-layouts  50.1 us (22%)
  other arithmetic  38 us (17%)
  between operations  14.2 us (6%)
  starting transfers between devices  6.7 us (3%)
  matrix products  4.01 us (2%)
    all_to_all x1, waiting for transfers between devices, shards(): lax.all_to_all(packed, 'tile', split_axis=2, concat_axis=2, tiled=True)  67.5 us
    all_gather x1, waiting for transfers between devices, shards(): member_piece = lax.all_gather(anomalies, 'mem', axis=0, tiled=True)  42.4 us
    gather x1, local copies, waits for them, and re-layouts, shards(): jnp.take(received, footprint.reshape(-1), axis=2)  24 us
    reduce_sum x1, other arithmetic, shards(): prior_out = jnp.sum(weighted, axis=3) + channel_bias[:, None, None]  19.8 us
    unnamed x17, local copies, waits for them, and re-layouts  16.6 us
    add x1, other arithmetic, shards(): prior_out = jnp.sum(weighted, axis=3) + channel_bias[:, None, None]  8.72 us
    all_to_all x1, starting transfers between devices, shards(): lax.all_to_all(packed, 'tile', split_axis=2, concat_axis=2, tiled=True)  6.67 us
    select_n x1, other arithmetic, shards(): packed = jnp.take(owned, slot_cols, axis=2)  6.6 us
  transfers between devices with their start and end apart: 2, of which 2 were waited for; matrix products, arithmetic and copies ran while one was open for 2% of the time, Pallas kernels for 0%

commit v1 on v0

v1 whole, which is shorter than its diff:
```python
import functools

import jax
import jax.numpy as jnp
from jax import lax
from jax.experimental import pallas as pl
from jax.experimental.pallas import tpu as pltpu
from jax.sharding import PartitionSpec as P

LANES = 128
SPLIT = (3, 3)


def one_hot(index, count, dtype=jnp.bfloat16):
    return (index[..., None] == lax.iota(jnp.int32, count)).astype(dtype)


def dot(spec, a, b):
    return jnp.einsum(spec, a, b, preferred_element_type=jnp.float32)


def pack_kernel(hot_ref, own_ref, *out_refs):
    packed = jnp.dot(
        hot_ref[...], own_ref[...], preferred_element_type=jnp.float32
    ).astype(jnp.bfloat16)
    slots = out_refs[0].shape[0]
    for d, out_ref in enumerate(out_refs):
        out_ref[...] = packed[d * slots : (d + 1) * slots]


def pack(hot, own, slots, first, block, count):
    columns_dev = own.shape[0]
    partners = hot.shape[0] // slots
    rows = count * block
    return list(
        pl.pallas_call(
            pack_kernel,
            grid=(count,),
            in_specs=[
                pl.BlockSpec(hot.shape, lambda i: (0, 0)),
                pl.BlockSpec((columns_dev, block), lambda i: (0, first + i)),
            ],
            out_specs=[pl.BlockSpec((slots, block), lambda i: (0, i))] * partners,
            out_shape=[jax.ShapeDtypeStruct((slots, rows), own.dtype)] * partners,
            cost_estimate=pl.CostEstimate(
                flops=2 * hot.size * rows,
                bytes_accessed=2 * rows * (columns_dev + hot.shape[0]),
                transcendentals=0,
            ),
            name="pack",
        )(hot, own)
    )


def prior_kernel(first, block, mem_dev, sources, bias_ref, spread_ref, *refs):
    out_ref = refs[-1]
    rows = jnp.concatenate([ref[...] for ref in refs[:sources]], axis=0)
    total = lax.dot_general(
        rows,
        spread_ref[...],
        (((0,), (0,)), ((), ())),
        preferred_element_type=jnp.float32,
    )
    channel = (first + pl.program_id(0)) * block
    for c in range(block):
        out_ref[c] = total[c * mem_dev : (c + 1) * mem_dev] + bias_ref[channel + c]


def prior_piece(shape, block, first, count, near, far, spread, bias, so_far):
    _, mem_dev, obs_count = shape
    width = block * mem_dev
    slots, all_slots = near[0].shape[0], spread.shape[0]
    in_specs = [
        pl.BlockSpec(memory_space=pltpu.SMEM),
        pl.BlockSpec(spread.shape, lambda i: (0, 0)),
        *[pl.BlockSpec((slots, width), lambda i: (0, first + i))] * len(near),
        *[pl.BlockSpec((far[0].shape[0], width), lambda i: (0, i))] * len(far),
    ]
    operands = [bias, spread, *near, *far]
    aliases = {}
    if so_far is not None:
        aliases = {len(operands): 0}
        in_specs.append(pl.BlockSpec(memory_space=pl.ANY))
        operands.append(so_far)
    return pl.pallas_call(
        functools.partial(prior_kernel, first, block, mem_dev, len(near) + len(far)),
        grid=(count,),
        in_specs=in_specs,
        out_specs=pl.BlockSpec((block, mem_dev, obs_count), lambda i: (first + i, 0, 0)),
        out_shape=jax.ShapeDtypeStruct(shape, jnp.float32),
        input_output_aliases=aliases,
        cost_estimate=pl.CostEstimate(
            flops=2 * all_slots * width * count * obs_count,
            bytes_accessed=2 * width * count * (all_slots + 2 * obs_count),
            transcendentals=0,
        ),
        name="prior",
    )(*operands)


def pieces_of(channels, mem_dev):
    for block in range(1, channels // 2 + 1):
        if channels % block == 0 and block * mem_dev % LANES == 0:
            total = channels // block
            relay = max(1, total * SPLIT[0] // sum(SPLIT))
            return block, relay, total - relay
    return channels, 1, 0


def shards(
    n_tile,
    n_mem,
    anomalies,
    analysis_weights,
    background_mean,
    background,
    jacobian_table,
    channel_list,
    send_slots,
    footprint,
    footprint_weight,
    channel_bias,
):
    mem_dev, _, columns_dev = anomalies.shape
    spectrum = jacobian_table.shape[0]
    channels = channel_list.shape[0]
    slots = send_slots.shape[2]
    obs_count, foot = footprint.shape
    half = n_tile // 2
    half_slots = half * slots
    me = lax.axis_index("tile")
    mine = lax.axis_index("mem")
    my_half = me // half
    halves = [[h * half + i for i in range(half)] for h in range(2)]
    mirror = [(i, (i + half) % n_tile) for i in range(n_tile)]
    block, relay, direct = pieces_of(channels, mem_dev)
    width = block * mem_dev

    place = me % half
    partners = jnp.stack([me ^ d for d in range(n_tile)])
    partner_cols = jnp.take(send_slots[0], partners, axis=0, mode="clip")
    far_cols = lax.dynamic_slice_in_dim(send_slots[0], (1 - my_half) * half, half, 0)
    relay_cols = lax.ppermute(far_cols, "tile", mirror)

    picks = one_hot(channel_list, spectrum)
    selected = dot("cs,sl->cl", picks, jacobian_table).astype(jnp.bfloat16)
    owned = dot("cl,klx->ckx", selected, background).astype(jnp.bfloat16)
    owned = owned.reshape(channels * mem_dev, columns_dev)
    identity = jnp.eye(columns_dev, dtype=jnp.bfloat16)
    hot = lax.optimization_barrier(one_hot(partner_cols.reshape(-1), columns_dev))
    relay_hot = lax.optimization_barrier(one_hot(relay_cols.reshape(-1), columns_dev))

    own = dot("sx,rx->sr", identity, owned[: relay * width]).astype(jnp.bfloat16)
    seen = lax.ppermute(own, "tile", mirror)
    own = dot("sx,rx->sr", identity, owned).astype(jnp.bfloat16)

    def to_partner(array, d):
        return lax.ppermute(array, "tile", [(i, i ^ d) for i in range(n_tile)])

    near = pack(hot[:half_slots], own, slots, 0, relay * width, 1 + (direct == relay))
    near[1:] = [to_partner(near[d], d) for d in range(1, half)]
    far = []
    if direct:
        far = pack(hot[half_slots:], own, slots, 1, relay * width, 1)
        far = [to_partner(far[d], half + d) for d in range(half)]

    places = footprint.T
    weights = footprint_weight.T
    near_place = places - my_half * half_slots
    far_place = places - (1 - my_half) * half_slots
    mixed_place = jnp.stack([near_place ^ (place * slots), far_place])
    spread = sum(
        jnp.where(
            mixed_place[:, None, j] == lax.iota(jnp.int32, half_slots)[None, :, None],
            weights[j],
            jnp.zeros((), weights.dtype),
        )
        for j in range(foot)
    ).reshape(2 * half_slots, obs_count)

    relayed = dot("sx,xr->sr", relay_hot, seen).astype(jnp.bfloat16)
    relayed = lax.all_to_all(
        relayed, "tile", 0, 0, tiled=True, axis_index_groups=halves
    )
    shape = (channels, mem_dev, obs_count)
    prior = None
    if direct:
        direct_spread = jnp.take(
            spread.reshape(n_tile, slots, obs_count),
            jnp.concatenate([jnp.arange(half), half + (jnp.arange(half) ^ place)]),
            axis=0,
            mode="clip",
        ).reshape(spread.shape)
        prior = prior_piece(
            shape, block, relay, direct, near, far, direct_spread, channel_bias, None
        )
    prior = prior_piece(
        shape, block, 0, relay, near, [relayed], spread, channel_bias, prior
    )

    weight_cols = lax.dynamic_slice_in_dim(analysis_weights[0], mine * mem_dev, mem_dev, 1)
    mixture = background_mean.astype(jnp.float32)[None]
    for shift in range(n_mem):
        piece = anomalies
        if shift:
            piece = lax.ppermute(
                anomalies, "mem", [((i + shift) % n_mem, i) for i in range(n_mem)]
            )
        start = lax.rem(mine + shift, n_mem) * mem_dev
        part = lax.dynamic_slice_in_dim(weight_cols, start, mem_dev, 0)
        mixture = mixture + dot("klc,km->mlc", piece, part)
    mixture = mixture.astype(jnp.bfloat16)
    return mixture, prior


def solution(mesh):
    sizes = dict(mesh.shape)
    placed = (
        P("mem", None, "tile"),
        P("tile", None, None),
        P(None, "tile"),
        P("mem", None, "tile"),
        P(),
        P(),
        P("tile", None, None),
        P("tile", None),
        P("tile", None),
        P(),
    )

    def body(*arrays):
        return shards(sizes["tile"], sizes["mem"], *arrays)

    return jax.shard_map(
        body,
        mesh=mesh,
        in_specs=placed,
        out_specs=(P("mem", None, "tile"), P(None, "mem", "tile")),
        check_vma=False,
    )
```

time: 224 us -> 136 us (0.61)
  the two profiles are of different devices: /device:TPU:11 before, /device:TPU:0 now
where the time goes in v1:
time: 136 us; the launch traced here: 135 us
  waiting for transfers between devices  53.1 us (39%)
  starting transfers between devices  31.1 us (23%)
  Pallas kernels  16.1 us (12%)
  matrix products  13.7 us (10%)
  local copies, waits for them, and re-layouts  12 us (9%)
  other arithmetic  7.8 us (6%)
    ppermute x15, waiting for transfers between devices, to_partner(): return lax.ppermute(array, 'tile', [(i, i ^ d) for i in range(n_tile)])  24.7 us
    ppermute x15, starting transfers between devices, to_partner(): return lax.ppermute(array, 'tile', [(i, i ^ d) for i in range(n_tile)])  22.7 us
    ppermute x1, waiting for transfers between devices, shards(): relay_cols = lax.ppermute(far_cols, 'tile', mirror)  17.4 us
    dot_general x6, matrix products, dot(): return jnp.einsum(spec, a, b, preferred_element_type=jnp.float32)  13.7 us
    ppermute x1, waiting for transfers between devices, shards(): seen = lax.ppermute(own, 'tile', mirror)  11 us
    pallas_call x2, Pallas kernels, prior_piece(): pl.pallas_call(functools.partial(prior_kernel, first, block, mem_dev, len...  10.8 us
    pallas_call x2, Pallas kernels, pack(): pl.pallas_call(pack_kernel, grid=(count,), in_specs=[pl.BlockSpec(hot.sha...  5.31 us
    add x2, other arithmetic, shards(): sum((jnp.where(mixed_place[:, None, j] == lax.iota(jnp.int32, half_slots)...  4.24 us
  transfers between devices with their start and end apart: 19, of which 10 were waited for; matrix products, arithmetic and copies ran while one was open for 18% of the time, Pallas kernels for 6%

profile of v1, /device:TPU:0, one launch (start us, length us, event | category | flops | bytes accessed | tf_op | source)
XLA Modules:
  0.0 134.6 jit_solution(12145641422726547144)
XLA Ops:
  0.8 1.4 %gather_fusion = s32[16,32]{1,0:T(8,128)S(1)} fusion(s32[16,32]{1,0:T(8,128)} %bitcast.108, s32[1024]{0:T(1024)S(1)} %pad_clamp_fusion.1), kind=kCustom, calls=%fused_computation | custom fusion | bytes 4160 | tf_op jit(solution)/shard_map/jit(_take)/gather | solution.py:141
  3.0 3.2 %fusion.4 = bf16[96,40,128]{2,0,1:T(8,128)(2,1)S(1)} fusion(bf16[40,137,128]{2,0,1:T(8,128)(2,1)} %param.13, bf16[8461,137]{0,1:T(8,128)(2,1)S(1)} %copy-done, s32[96]{0:T(128)} %param.15), kind=kOutput, calls=%fused_computation.11 | convolution fusion | flops 358551552 | bytes 4704618 | tf_op jit(solution)/shard_map/cl,klx->ckx/dot_general | solution.py:19
  6.6 1.4 %convolution_convert_fusion.own_ref = bf16[128,3840]{1,0:T(8,128)(2,1)} fusion(bf16[3840,128]{1,0:T(8,128)(2,1)S(1)} %bitcast.105), kind=kOutput, calls=%fused_computation.2 | convolution fusion | flops 126337024 | bytes 1966080 | tf_op jit(solution)/shard_map/sx,rx->sr/dot_general | solution.py:19
  8.0 2.5 %pack.3 = (bf16[32,1920]{1,0:T(8,128)(2,1)}, bf16[32,1920]{1,0:T(8,128)(2,1)}, bf16[32,1920]{1,0:T(8,128)(2,1)}, bf16[32,1920]{1,0:T(8,128)(2,1)}, bf16[32,1920]...) custom-call(bf16[256,128]{1,0:T(8,128)(2,1)} %get-tuple-element.38.hot_ref, ...), custom_call_target="tpu_custom_call" | custom-call | flops 125829120 | bytes 1474560 | tf_op jit(solution)/shard_map/pack/pallas_call | solution.py:36
  10.5 4.1 %collective-permute-start.10 = (bf16[32,1920]{1,0:T(8,128)(2,1)}, bf16[32,1920]{1,0:T(8,128)(2,1)}, u32[]{:S(2)}, u32[]{:S(2)}) collective-permute-start(bf16[32,1920]{1,0:T(8,128)(2,1)} %get-tuple-element.26), channel_id=1, source_target_pairs={{0,16},{2,18},{4,20},{6,22},{8,24},{10,26},{12,28},{14,30},{16,0},... | collective-permute-start | bytes 368648 | tf_op jit(solution)/shard_map/ppermute | solution.py:158
  14.6 3.0 %collective-permute-start.12 = (bf16[32,1920]{1,0:T(8,128)(2,1)}, bf16[32,1920]{1,0:T(8,128)(2,1)}, u32[]{:S(2)}, u32[]{:S(2)}) collective-permute-start(bf16[32,1920]{1,0:T(8,128)(2,1)} %get-tuple-element.28), channel_id=1, source_target_pairs={{0,20},{2,22},{4,16},{6,18},{8,28},{10,30},{12,24},{14,26},{16,4},... | collective-permute-start | bytes 368648 | tf_op jit(solution)/shard_map/ppermute | solution.py:158
  19.5 2.1 %collective-permute-start.9 = (bf16[128,1920]{1,0:T(8,128)(2,1)S(1)}, bf16[128,1920]{1,0:T(8,128)(2,1)S(1)}, u32[]{:S(2)}, u32[]{:S(2)}) collective-permute-start(bf16[128,1920]{1,0:T(8,128)(2,1)S(1)} %convolution_convert_fusion.2), channel_id=1, source_target_pairs={{0,16},{2,18},{4,20},{6,22},{8,24},{10,26},{12,28},{14,30},{16,0},... | collective-permute-start | bytes 1474568 | tf_op jit(solution)/shard_map/ppermute | solution.py:154
  23.5 1.4 %slice_reduce_fusion.3 = (bf16[512]{0:T(512)(128)(2,1)}, bf16[512]{0:T(512)(128)(2,1)}, bf16[512]{0:T(512)(128)(2,1)}, bf16[512]{0:T(512)(128)(2,1)}) fusion(bf16[4,512]{1,0:T(4,128)(2,1)} %bitcast.109), kind=kLoop, calls=%fused_computation.70 | loop fusion | bytes 8192 | tf_op jit(solution)/shard_map/slice | solution.py:175
  25.5 17.4 %collective-permute-done.8 = s32[8,32]{1,0:T(8,128)} collective-permute-done((s32[8,32]{1,0:T(8,128)}, s32[8,32]{1,0:T(8,128)}, u32[]{:S(2)}, u32[]{:S(2)}) %collective-permute-start.8) | collective-permute-done | bytes 1056 | tf_op jit(solution)/shard_map/ppermute | solution.py:143
  45.0 11.0 %collective-permute-done.9 = bf16[128,1920]{1,0:T(8,128)(2,1)S(1)} collective-permute-done((bf16[128,1920]{1,0:T(8,128)(2,1)S(1)}, bf16[128,1920]{1,0:T(8,128)(2,1)S(1)}, u32[]{:S(2)}, u32[]{:S(2)}) %collective-permute-start.9) | collective-permute-done | bytes 491552 | tf_op jit(solution)/shard_map/ppermute | solution.py:154
  56.0 1.8 %collective-permute-start = (bf16[40,137,128]{2,0,1:T(8,128)(2,1)}, bf16[40,137,128]{2,0,1:T(8,128)(2,1)}, u32[]{:S(2)}, u32[]{:S(2)}) collective-permute-start(bf16[40,137,128]{2,0,1:T(8,128)(2,1)} %param.10), channel_id=1, source_target_pairs={{1,0},{0,1},{3,2},{2,3},{5,4},{4,5},{7,6},{6,7},{9,8},{8,9},{11,10... | collective-permute-start | bytes 4208648 | tf_op jit(solution)/shard_map/ppermute | solution.py:206
  57.8 1.4 %convolution_convert_fusion.1 = bf16[256,1920]{1,0:T(8,128)(2,1)} fusion(bf16[256,128]{1,0:T(8,128)(2,1)S(1)} %fusion.20, bf16[128,1920]{1,0:T(8,128)(2,1)S(1)} %collective-permute-done.9), kind=kOutput, calls=%fused_computation.6 | convolution fusion | flops 126320640 | bytes 1540096 | tf_op jit(solution)/shard_map/sx,xr->sr/dot_general | solution.py:19
  59.2 3.6 %all-to-all-start = ((bf16[8,32,1920]{2,1,0:T(8,128)(2,1)}), bf16[8,32,1920]{2,1,0:T(8,128)(2,1)S(1)}, u32[]{:S(2)}, u32[]{:S(2)}) async-start(bf16[8,32,1920]{2,1,0:T(8,128)(2,1)} %bitcast.104), calls=%async_computation | async-start | bytes 1966080 | tf_op jit(solution)/shard_map/all_to_all | solution.py:182
  63.4 2.2 %fusion.15 = bf16[16,32,512]{2,1,0:T(8,128)(2,1)} fusion(s32[16,512]{1,0:T(8,128)S(1)} %broadcast_bitcast_fusion, s32[16,512]{1,0:T(8,128)S(1)} %broadcast_bitcast_fusion.1, s32[16,512]{1,0:T(8,128)S(1)} %broadcast_bitcast_fusion.2, s32[16,32]{1,0:T(8,128)S(1)} %broadcast_bitcast_fusion.4, s32[16,512]{1,0:T(8,128)} %broadcast_bitcast_fusion.3, ...), kind=kLoop, calls=%fused_computation.28 | loop fusion | flops 2883584 | bytes 661504 | tf_op jit(solution)/shard_map/add | solution.py:172
  65.6 3.1 %collective-permute-start.14 = (bf16[32,1920]{1,0:T(8,128)(2,1)}, bf16[32,1920]{1,0:T(8,128)(2,1)}, u32[]{:S(2)}, u32[]{:S(2)}) collective-permute-start(bf16[32,1920]{1,0:T(8,128)(2,1)} %get-tuple-element.30), channel_id=1, source_target_pairs={{0,24},{2,26},{4,28},{6,30},{8,16},{10,18},{12,20},{14,22},{16,8},... | collective-permute-start | bytes 368648 | tf_op jit(solution)/shard_map/ppermute | solution.py:158
  69.2 3.8 %collective-permute-start.16 = (bf16[32,1920]{1,0:T(8,128)(2,1)}, bf16[32,1920]{1,0:T(8,128)(2,1)}, u32[]{:S(2)}, u32[]{:S(2)}) collective-permute-start(bf16[32,1920]{1,0:T(8,128)(2,1)} %get-tuple-element.32), channel_id=1, source_target_pairs={{0,28},{2,30},{4,24},{6,26},{8,20},{10,22},{12,16},{14,18},{16,12}... | collective-permute-start | bytes 368648 | tf_op jit(solution)/shard_map/ppermute | solution.py:158
  72.9 2.8 %pack.2 = (bf16[32,3840]{1,0:T(8,128)(2,1)}, bf16[32,3840]{1,0:T(8,128)(2,1)}, bf16[32,3840]{1,0:T(8,128)(2,1)}, bf16[32,3840]{1,0:T(8,128)(2,1)}, bf16[32,3840]...) custom-call(bf16[256,128]{1,0:T(8,128)(2,1)} %get-tuple-element.39.hot_ref, ...), custom_call_target="tpu_custom_call" | custom-call | flops 251658240 | bytes 2949120 | tf_op jit(solution)/shard_map/pack/pallas_call | solution.py:36
  76.2 4.8 %collective-permute-done.14.refs_12_ = bf16[32,1920]{1,0:T(8,128)(2,1)} collective-permute-done((bf16[32,1920]{1,0:T(8,128)(2,1)}, bf16[32,1920]{1,0:T(8,128)(2,1)}, u32[]{:S(2)}, u32[]{:S(2)}) %collective-permute-start.14) | collective-permute-done | bytes 122912 | tf_op jit(solution)/shard_map/ppermute | solution.py:158
  81.1 1.5 %collective-permute-start.2 = (bf16[32,3840]{1,0:T(8,128)(2,1)}, bf16[32,3840]{1,0:T(8,128)(2,1)}, u32[]{:S(2)}, u32[]{:S(2)}) collective-permute-start(bf16[32,3840]{1,0:T(8,128)(2,1)} %get-tuple-element.20), channel_id=1, source_target_pairs={{0,4},{2,6},{4,0},{6,2},{8,12},{10,14},{12,8},{14,10},{16,20},{18,... | collective-permute-start | bytes 737288 | tf_op jit(solution)/shard_map/ppermute | solution.py:158
  82.5 2.0 %collective-permute-start.3 = (bf16[32,3840]{1,0:T(8,128)(2,1)}, bf16[32,3840]{1,0:T(8,128)(2,1)}, u32[]{:S(2)}, u32[]{:S(2)}) collective-permute-start(bf16[32,3840]{1,0:T(8,128)(2,1)} %get-tuple-element.21), channel_id=1, source_target_pairs={{0,6},{2,4},{4,2},{6,0},{8,14},{10,12},{12,10},{14,8},{16,22},{18,... | collective-permute-start | bytes 737288 | tf_op jit(solution)/shard_map/ppermute | solution.py:158
  84.6 2.2 %collective-permute-done.16.refs_14_ = bf16[32,1920]{1,0:T(8,128)(2,1)} collective-permute-done((bf16[32,1920]{1,0:T(8,128)(2,1)}, bf16[32,1920]{1,0:T(8,128)(2,1)}, u32[]{:S(2)}, u32[]{:S(2)}) %collective-permute-start.16) | collective-permute-done | bytes 122912 | tf_op jit(solution)/shard_map/ppermute | solution.py:158
  87.6 2.1 %fusion.16.spread_ref = bf16[512,512]{1,0:T(8,128)(2,1)} fusion(s32[2,512]{1,0:T(2,128)S(1)} %get-tuple-element.46, s32[2,512]{1,0:T(2,128)} %copy-done.3, s32[2,512]{1,0:T(2,128)} %copy-done.4, s32[512]{0:T(512)S(1)} %bitcast.110, s32[2,512]{1,0:T(2,128)} %copy-done.5, bf16[512]{0:T(512)(128)(2,1)} %get-tuple-element.35, ...), kind=kLoop, calls=%fused_computation.29 | loop fusion | flops 2883584 | bytes 546816 | tf_op jit(solution)/shard_map/add | solution.py:172
  91.2 2.4 %gather_fusion.1 = bf16[16,32,512]{2,1,0:T(8,128)(2,1)} fusion(bf16[16,32,512]{2,1,0:T(8,128)(2,1)} %fusion.15, s32[1024]{0:T(1024)S(1)} %pad_clamp_fusion), kind=kCustom, calls=%fused_computation.1 | custom fusion | bytes 1048640 | tf_op jit(solution)/shard_map/jit(_take)/gather | solution.py:188
  93.6 1.5 %collective-permute-done.17.refs_15_ = bf16[32,1920]{1,0:T(8,128)(2,1)} collective-permute-done((bf16[32,1920]{1,0:T(8,128)(2,1)}, bf16[32,1920]{1,0:T(8,128)(2,1)}, u32[]{:S(2)}, u32[]{:S(2)}) %collective-permute-start.17) | collective-permute-done | bytes 122912 | tf_op jit(solution)/shard_map/ppermute | solution.py:158
  97.5 2.0 %collective-permute-start.7 = (bf16[32,3840]{1,0:T(8,128)(2,1)}, bf16[32,3840]{1,0:T(8,128)(2,1)}, u32[]{:S(2)}, u32[]{:S(2)}) collective-permute-start(bf16[32,3840]{1,0:T(8,128)(2,1)} %get-tuple-element.25), channel_id=1, source_target_pairs={{0,14},{2,12},{4,10},{6,8},{8,6},{10,4},{12,2},{14,0},{16,30},{18,... | collective-permute-start | bytes 737288 | tf_op jit(solution)/shard_map/ppermute | solution.py:158
  99.5 3.5 %fusion.22 = f32[40,137,128]{2,0,1:T(8,128)} fusion(bf16[40,137,128]{2,0,1:T(8,128)(2,1)} %param.10, bf16[1,80,80]{2,1,0:T(8,128)(2,1)S(1)} %copy-done.6, s32[]{:T(128)S(6)} %select_n.59, s32[]{:T(128)S(6)} %select_n.61), kind=kOutput, calls=%fused_computation.48 | convolution fusion | flops 56115200 | bytes 4218888 | tf_op jit(solution)/shard_map/klc,km->mlc/dot_general | solution.py:19
  104.2 2.8 %collective-permute-done.5.refs_5_ = bf16[32,3840]{1,0:T(8,128)(2,1)} collective-permute-done((bf16[32,3840]{1,0:T(8,128)(2,1)}, bf16[32,3840]{1,0:T(8,128)(2,1)}, u32[]{:S(2)}, u32[]{:S(2)}) %collective-permute-start.5) | collective-permute-done | bytes 245792 | tf_op jit(solution)/shard_map/ppermute | solution.py:158
  107.0 7.7 %collective-permute-done.6.refs_6_ = bf16[32,3840]{1,0:T(8,128)(2,1)} collective-permute-done((bf16[32,3840]{1,0:T(8,128)(2,1)}, bf16[32,3840]{1,0:T(8,128)(2,1)}, u32[]{:S(2)}, u32[]{:S(2)}) %collective-permute-start.6) | collective-permute-done | bytes 245792 | tf_op jit(solution)/shard_map/ppermute | solution.py:158
  114.7 4.1 %collective-permute-done.7.refs_7_ = bf16[32,3840]{1,0:T(8,128)(2,1)} collective-permute-done((bf16[32,3840]{1,0:T(8,128)(2,1)}, bf16[32,3840]{1,0:T(8,128)(2,1)}, u32[]{:S(2)}, u32[]{:S(2)}) %collective-permute-start.7) | collective-permute-done | bytes 245792 | tf_op jit(solution)/shard_map/ppermute | solution.py:158
  118.8 5.4 %prior.2.refs_9_ = f32[96,40,512]{2,1,0:T(8,128)} custom-call(f32[96]{0:T(128)} %bias_ref.3, bf16[512,512]{1,0:T(8,128)(2,1)} %bitcast.106, bf16[32,3840]{1,0:T(8,128)(2,1)} %get-tuple-element.18.refs_0_, bf16[32,3840]{1,0:T(8,128)(2,1)} %collective-permute-done.1.refs_1_, bf16[32,3840]{1,0:T(8,128)(2,1)} %collective-permute-done.2.refs_2_, ...), custom_call_target="tpu_custom_call" | custom-call | flops 1006632960 | bytes 5898240 | tf_op jit(solution)/shard_map/prior/pallas_call | solution.py:85
  124.3 4.0 %add_convert_fusion = bf16[40,137,128]{2,0,1:T(8,128)(2,1)} fusion(f32[40,137,128]{2,0,1:T(8,128)} %fusion.22, bf16[40,137,128]{2,0,1:T(8,128)(2,1)} %collective-permute-done, f32[137,128]{1,0:T(8,128)S(1)} %convert_element_type.29, bf16[1,80,80]{2,1,0:T(8,128)(2,1)S(1)} %copy-done.6, s32[]{:T(128)S(6)} %select_n.63, s32[]{:T(128)S(6)} %select_n.61), kind=kOutput, calls=%fused_computation.5 | convolution fusion | flops 58219520 | bytes 5695496 | tf_op jit(solution)/shard_map/klc,km->mlc/dot_general | solution.py:19
  129.2 5.4 %prior.3 = f32[96,40,512]{2,1,0:T(8,128)} custom-call(f32[96]{0:T(128)} %bias_ref.3, bf16[512,512]{1,0:T(8,128)(2,1)} %fusion.16.spread_ref, bf16[32,3840]{1,0:T(8,128)(2,1)} %get-tuple-element.18.refs_0_, bf16[32,3840]{1,0:T(8,128)(2,1)} %collective-permute-done.1.refs_1_, ...), custom_call_target="tpu_custom_call", output_to_operand_aliasing={{}: (11, {})} | custom-call | flops 1006632960 | bytes 5898240 | tf_op jit(solution)/shard_map/prior/pallas_call | solution.py:85
  (65 shorter events, 16.3 us)
Async XLA Ops:
  0.6 2.4 %copy-start = (bf16[8461,137]{0,1:T(8,128)(2,1)S(1)}, bf16[8461,137]{0,1:T(8,128)(2,1)}, u32[]{:S(2)}) copy-start(bf16[8461,137]{0,1:T(8,128)(2,1)} %param.14) | copy-start | bytes 6954946
  6.6 10.9 %copy-start.2 = (s32[1,16,32]{2,1,0:T(8,128)S(1)}, s32[1,16,32]{2,1,0:T(8,128)}, u32[]{:S(2)}) copy-start(s32[1,16,32]{2,1,0:T(8,128)} %param.16) | copy-start | bytes 6148
  8.0 13.6 %copy-start.7 = (s32[512,4]{0,1:T(4,128)S(1)}, s32[512,4]{0,1:T(4,128)}, u32[]{:S(2)}) copy-start(s32[512,4]{0,1:T(4,128)} %param.17) | copy-start | bytes 24580
  10.5 55.1 %collective-permute-start.10 = (bf16[32,1920]{1,0:T(8,128)(2,1)}, bf16[32,1920]{1,0:T(8,128)(2,1)}, u32[]{:S(2)}, u32[]{:S(2)}) collective-permute-start(bf16[32,1920]{1,0:T(8,128)(2,1)} %get-tuple-element.26), channel_id=1, source_target_pairs={{0,16},{2,18},{4,20},{6,22},{8,24},{10,26},{12,28},{14,30},{16,0},... | collective-permute-start | bytes 368648 | tf_op jit(solution)/shard_map/ppermute | solution.py:158
  14.6 54.2 %collective-permute-start.11 = (bf16[32,1920]{1,0:T(8,128)(2,1)}, bf16[32,1920]{1,0:T(8,128)(2,1)}, u32[]{:S(2)}, u32[]{:S(2)}) collective-permute-start(bf16[32,1920]{1,0:T(8,128)(2,1)} %get-tuple-element.27), channel_id=1, source_target_pairs={{0,18},{2,16},{4,22},{6,20},{8,26},{10,24},{12,30},{14,28},{16,2},... | collective-permute-start | bytes 368648 | tf_op jit(solution)/shard_map/ppermute | solution.py:158
  14.6 54.6 %collective-permute-start.12 = (bf16[32,1920]{1,0:T(8,128)(2,1)}, bf16[32,1920]{1,0:T(8,128)(2,1)}, u32[]{:S(2)}, u32[]{:S(2)}) collective-permute-start(bf16[32,1920]{1,0:T(8,128)(2,1)} %get-tuple-element.28), channel_id=1, source_target_pairs={{0,20},{2,22},{4,16},{6,18},{8,28},{10,30},{12,24},{14,26},{16,4},... | collective-permute-start | bytes 368648 | tf_op jit(solution)/shard_map/ppermute | solution.py:158
  18.2 24.8 %collective-permute-start.8 = (s32[8,32]{1,0:T(8,128)}, s32[8,32]{1,0:T(8,128)}, u32[]{:S(2)}, u32[]{:S(2)}) collective-permute-start(s32[8,32]{1,0:T(8,128)} %dynamic-slice_bitcast_fusion), channel_id=1, source_target_pairs={{0,16},{2,18},{4,20},{6,22},{8,24},{10,26},{12,28},{14,30},{16,0},... | collective-permute-start | bytes 3080 | tf_op jit(solution)/shard_map/ppermute | solution.py:143
  19.5 36.5 %collective-permute-start.9 = (bf16[128,1920]{1,0:T(8,128)(2,1)S(1)}, bf16[128,1920]{1,0:T(8,128)(2,1)S(1)}, u32[]{:S(2)}, u32[]{:S(2)}) collective-permute-start(bf16[128,1920]{1,0:T(8,128)(2,1)S(1)} %convolution_convert_fusion.2), channel_id=1, source_target_pairs={{0,16},{2,18},{4,20},{6,22},{8,24},{10,26},{12,28},{14,30},{16,0},... | collective-permute-start | bytes 1474568 | tf_op jit(solution)/shard_map/ppermute | solution.py:154
  21.7 0.6 copy-start.3
  22.3 0.6 copy-start.4
  22.3 0.6 copy-start.5
  42.9 32.8 %collective-permute-start.13 = (bf16[32,1920]{1,0:T(8,128)(2,1)}, bf16[32,1920]{1,0:T(8,128)(2,1)}, u32[]{:S(2)}, u32[]{:S(2)}) collective-permute-start(bf16[32,1920]{1,0:T(8,128)(2,1)} %get-tuple-element.29), channel_id=1, source_target_pairs={{0,22},{2,20},{4,18},{6,16},{8,30},{10,28},{12,26},{14,24},{16,6},... | collective-permute-start | bytes 368648 | tf_op jit(solution)/shard_map/ppermute | solution.py:158
  56.0 68.3 %collective-permute-start = (bf16[40,137,128]{2,0,1:T(8,128)(2,1)}, bf16[40,137,128]{2,0,1:T(8,128)(2,1)}, u32[]{:S(2)}, u32[]{:S(2)}) collective-permute-start(bf16[40,137,128]{2,0,1:T(8,128)(2,1)} %param.10), channel_id=1, source_target_pairs={{1,0},{0,1},{3,2},{2,3},{5,4},{4,5},{7,6},{6,7},{9,8},{8,9},{11,10... | collective-permute-start | bytes 4208648 | tf_op jit(solution)/shard_map/ppermute | solution.py:206
  59.2 69.1 %all-to-all-start = ((bf16[8,32,1920]{2,1,0:T(8,128)(2,1)}), bf16[8,32,1920]{2,1,0:T(8,128)(2,1)S(1)}, u32[]{:S(2)}, u32[]{:S(2)}) async-start(bf16[8,32,1920]{2,1,0:T(8,128)(2,1)} %bitcast.104), calls=%async_computation | async-start | bytes 1966080 | tf_op jit(solution)/shard_map/all_to_all | solution.py:182
  65.6 33.9 %copy-start.6 = (bf16[1,80,80]{2,1,0:T(8,128)(2,1)S(1)}, bf16[1,80,80]{2,1,0:T(8,128)(2,1)}, u32[]{:S(2)}) copy-start(bf16[1,80,80]{2,1,0:T(8,128)(2,1)} %param.11) | copy-start | bytes 38404
  65.6 15.5 %collective-permute-start.14 = (bf16[32,1920]{1,0:T(8,128)(2,1)}, bf16[32,1920]{1,0:T(8,128)(2,1)}, u32[]{:S(2)}, u32[]{:S(2)}) collective-permute-start(bf16[32,1920]{1,0:T(8,128)(2,1)} %get-tuple-element.30), channel_id=1, source_target_pairs={{0,24},{2,26},{4,28},{6,30},{8,16},{10,18},{12,20},{14,22},{16,8},... | collective-permute-start | bytes 368648 | tf_op jit(solution)/shard_map/ppermute | solution.py:158
  68.7 13.8 %collective-permute-start.15 = (bf16[32,1920]{1,0:T(8,128)(2,1)}, bf16[32,1920]{1,0:T(8,128)(2,1)}, u32[]{:S(2)}, u32[]{:S(2)}) collective-permute-start(bf16[32,1920]{1,0:T(8,128)(2,1)} %get-tuple-element.31), channel_id=1, source_target_pairs={{0,26},{2,24},{4,30},{6,28},{8,18},{10,16},{12,22},{14,20},{16,10}... | collective-permute-start | bytes 368648 | tf_op jit(solution)/shard_map/ppermute | solution.py:158
  69.2 17.6 %collective-permute-start.16 = (bf16[32,1920]{1,0:T(8,128)(2,1)}, bf16[32,1920]{1,0:T(8,128)(2,1)}, u32[]{:S(2)}, u32[]{:S(2)}) collective-permute-start(bf16[32,1920]{1,0:T(8,128)(2,1)} %get-tuple-element.32), channel_id=1, source_target_pairs={{0,28},{2,30},{4,24},{6,26},{8,20},{10,22},{12,16},{14,18},{16,12}... | collective-permute-start | bytes 368648 | tf_op jit(solution)/shard_map/ppermute | solution.py:158
  75.7 19.3 %collective-permute-start.1 = (bf16[32,3840]{1,0:T(8,128)(2,1)}, bf16[32,3840]{1,0:T(8,128)(2,1)}, u32[]{:S(2)}, u32[]{:S(2)}) collective-permute-start(bf16[32,3840]{1,0:T(8,128)(2,1)} %get-tuple-element.19), channel_id=1, source_target_pairs={{0,2},{2,0},{4,6},{6,4},{8,10},{10,8},{12,14},{14,12},{16,18},{18,... | collective-permute-start | bytes 737288 | tf_op jit(solution)/shard_map/ppermute | solution.py:158
  81.1 14.9 %collective-permute-start.2 = (bf16[32,3840]{1,0:T(8,128)(2,1)}, bf16[32,3840]{1,0:T(8,128)(2,1)}, u32[]{:S(2)}, u32[]{:S(2)}) collective-permute-start(bf16[32,3840]{1,0:T(8,128)(2,1)} %get-tuple-element.20), channel_id=1, source_target_pairs={{0,4},{2,6},{4,0},{6,2},{8,12},{10,14},{12,8},{14,10},{16,20},{18,... | collective-permute-start | bytes 737288 | tf_op jit(solution)/shard_map/ppermute | solution.py:158
  82.5 15.0 %collective-permute-start.3 = (bf16[32,3840]{1,0:T(8,128)(2,1)}, bf16[32,3840]{1,0:T(8,128)(2,1)}, u32[]{:S(2)}, u32[]{:S(2)}) collective-permute-start(bf16[32,3840]{1,0:T(8,128)(2,1)} %get-tuple-element.21), channel_id=1, source_target_pairs={{0,6},{2,4},{4,2},{6,0},{8,14},{10,12},{12,10},{14,8},{16,22},{18,... | collective-permute-start | bytes 737288 | tf_op jit(solution)/shard_map/ppermute | solution.py:158
  86.7 8.3 %collective-permute-start.17 = (bf16[32,1920]{1,0:T(8,128)(2,1)}, bf16[32,1920]{1,0:T(8,128)(2,1)}, u32[]{:S(2)}, u32[]{:S(2)}) collective-permute-start(bf16[32,1920]{1,0:T(8,128)(2,1)} %get-tuple-element.33), channel_id=1, source_target_pairs={{0,30},{2,28},{4,26},{6,24},{8,22},{10,20},{12,18},{14,16},{16,14}... | collective-permute-start | bytes 368648 | tf_op jit(solution)/shard_map/ppermute | solution.py:158
  95.1 9.1 %collective-permute-start.4 = (bf16[32,3840]{1,0:T(8,128)(2,1)}, bf16[32,3840]{1,0:T(8,128)(2,1)}, u32[]{:S(2)}, u32[]{:S(2)}) collective-permute-start(bf16[32,3840]{1,0:T(8,128)(2,1)} %get-tuple-element.22), channel_id=1, source_target_pairs={{0,8},{2,10},{4,12},{6,14},{8,0},{10,2},{12,4},{14,6},{16,24},{18,... | collective-permute-start | bytes 737288 | tf_op jit(solution)/shard_map/ppermute | solution.py:158
  95.1 11.9 %collective-permute-start.5 = (bf16[32,3840]{1,0:T(8,128)(2,1)}, bf16[32,3840]{1,0:T(8,128)(2,1)}, u32[]{:S(2)}, u32[]{:S(2)}) collective-permute-start(bf16[32,3840]{1,0:T(8,128)(2,1)} %get-tuple-element.23), channel_id=1, source_target_pairs={{0,10},{2,8},{4,14},{6,12},{8,2},{10,0},{12,6},{14,4},{16,26},{18,... | collective-permute-start | bytes 737288 | tf_op jit(solution)/shard_map/ppermute | solution.py:158
  96.0 18.7 %collective-permute-start.6 = (bf16[32,3840]{1,0:T(8,128)(2,1)}, bf16[32,3840]{1,0:T(8,128)(2,1)}, u32[]{:S(2)}, u32[]{:S(2)}) collective-permute-start(bf16[32,3840]{1,0:T(8,128)(2,1)} %get-tuple-element.24), channel_id=1, source_target_pairs={{0,12},{2,14},{4,8},{6,10},{8,4},{10,6},{12,0},{14,2},{16,28},{18,... | collective-permute-start | bytes 737288 | tf_op jit(solution)/shard_map/ppermute | solution.py:158
  97.5 21.4 %collective-permute-start.7 = (bf16[32,3840]{1,0:T(8,128)(2,1)}, bf16[32,3840]{1,0:T(8,128)(2,1)}, u32[]{:S(2)}, u32[]{:S(2)}) collective-permute-start(bf16[32,3840]{1,0:T(8,128)(2,1)} %get-tuple-element.25), channel_id=1, source_target_pairs={{0,14},{2,12},{4,10},{6,8},{8,6},{10,4},{12,2},{14,0},{16,30},{18,... | collective-permute-start | bytes 737288 | tf_op jit(solution)/shard_map/ppermute | solution.py:158
  128.3 1.0 copy-start.1
